TPU v7x, 128 devices: a whole 4x4x4 slice. The times are simulated.
128 devices in a mesh: row: 8 (over x, y_hi), col: 16 (over z, y_lo, core).
Axes of the slice: x: 4, y: 4 (y_hi: 2, y_lo: 2; y = y_hi * 2 + y_lo), z: 4, core: 2. Of those that a mesh axis runs over, the one named last changes fastest.
Arguments:
- voltages: bfloat16 [4096, 64, 2, 256], P(('col', 'row')), may hold values from -6 to 6
- auto_prev: float32 [64, 4096], P('row', 'col'), may hold values from 0.5 to 8
- station_order: int32 [4096], replicated, may hold values from 0 to 4095, each once
Outputs:
- visibilities: bfloat16 [64, 9, 4096, 512], P('row', None, 'col')
Inputs may be any that keep to these rules, and one draw needn't show every extreme that they name: `station_order`: a permutation of the block positions.
All inputs are finite; a program needn't handle non-finite values.
Results may differ from a plain program's by a relative error of at most 0.001.
Values may be sent and summed in bfloat16 or wider, within the bound.
A program may use at most 128 MiB of HBM per device.

v0:
```python
import jax
import jax.numpy as jnp
from jax import lax
from jax.sharding import PartitionSpec as P

SAMPLES = 256


def laid_out(parts, dim):
    parts = jnp.moveaxis(parts, 0, dim)
    shape = parts.shape
    return parts.reshape(*shape[:dim], shape[dim] * shape[dim + 1], *shape[dim + 2 :])


def copy_for_each(value, axis):
    count = lax.axis_size(axis)
    return lax.all_to_all(
        jnp.broadcast_to(value[None], (count, *value.shape)), axis, 0, 0, tiled=True
    )


def gather_directly(value, axis, dim):
    return laid_out(copy_for_each(value, axis), dim)


def from_behind(value, axis, by):
    count = lax.axis_size(axis)
    return lax.ppermute(value, axis, [(i, (i + by) % count) for i in range(count)])


def per_device(voltages, auto_prev, station_order):
    local = lax.all_to_all(voltages, "row", split_axis=1, concat_axis=0, tiled=True)
    block_size, chan_count, _, sample_count = local.shape
    blocks_count = lax.axis_size("col")
    offsets = blocks_count // 2 + 1
    block_index = lax.axis_index("col")
    autos_all = gather_directly(auto_prev, "col", 1)
    inverse = 1.0 / jnp.sqrt(jnp.take(autos_all, station_order, axis=1))
    row_scale = lax.dynamic_slice_in_dim(inverse, block_index * block_size, block_size, 1)
    own_rows = jnp.transpose(local.reshape(block_size, chan_count, 2 * sample_count), (1, 0, 2))
    own_turned = jnp.concatenate(
        [own_rows[:, :, sample_count:], -own_rows[:, :, :sample_count]], axis=-1
    )
    tiles = []
    partner = own_rows
    for offset in range(offsets):
        if offset > 0:
            partner = from_behind(partner, "col", 1)
        real_part = jnp.einsum(
            "cih,cjh->cij", own_rows, partner, preferred_element_type=jnp.float32
        )
        imag_part = jnp.einsum(
            "cih,cjh->cij", own_turned, partner, preferred_element_type=jnp.float32
        )
        start = (block_index - offset) % blocks_count * block_size
        column_scale = lax.dynamic_slice_in_dim(inverse, start, block_size, 1)
        factor = row_scale[:, :, None] * column_scale[:, None, :] * (1.0 / SAMPLES)
        tiles.append(
            jnp.concatenate([real_part * factor, imag_part * factor], axis=-1).astype(jnp.bfloat16)
        )
    return jnp.stack(tiles, axis=1)


def solution(mesh):
    return jax.shard_map(
        per_device,
        mesh=mesh,
        in_specs=(P(("col", "row"), None, None, None), P("row", "col"), P()),
        out_specs=P("row", None, "col", None),
        check_vma=False,
    )
```

profile of v0, /device:TPU:0, one launch (start us, length us, event | category | flops | bytes accessed | tf_op | source)
XLA Modules:
  0.0 298.5 jit_solution(4134258130890512091)
XLA Ops:
  0.0 3.9 %copy.17 = bf16[32,64,2,256]{3,2,0,1:T(2,128)(2,1)S(1)} copy(bf16[32,64,2,256]{3,2,1,0:T(2,128)(2,1)} %param.3) | data formatting | bytes 4194304 | tf_op args[0]
  3.9 34.9 %all_to_all.20 = bf16[32,64,2,256]{3,2,0,1:T(2,128)(2,1)S(1)} all-to-all(bf16[32,64,2,256]{3,2,0,1:T(2,128)(2,1)S(1)} %copy.17), channel_id=1, replica_groups=mesh['row'=8,'col'=16] {'row'}, dimensions={1} | all-to-all | bytes 4194304 | tf_op jit(solution)/shard_map/all_to_all | solution.py:32
  38.8 4.4 %copy.32 = bf16[32,8,8,2,256]{4,3,0,1,2:T(2,128)(2,1)} copy(bf16[32,8,8,2,256]{4,3,0,2,1:T(2,128)(2,1)S(1)} %bitcast.103) | data formatting | bytes 4194304 | tf_op jit(solution)/shard_map/all_to_all | solution.py:32
  43.3 3.2 %reshape.302 = bf16[256,8,512]{2,0,1:T(8,128)(2,1)S(1)} reshape(bf16[8,32,8,2,256]{4,3,1,0,2:T(2,128)(2,1)} %bitcast.104) | data formatting | bytes 4194304 | tf_op jit(solution)/shard_map/reshape | solution.py:40
  46.5 27.6 %collective-permute-done = bf16[8,256,512]{2,1,0:T(8,128)(2,1)S(1)} collective-permute-done((bf16[8,256,512]{2,1,0:T(8,128)(2,1)S(1)}, bf16[8,256,512]{2,1,0:T(8,128)(2,1)S(1)}, u32[]{:S(2)}, u32[]{:S(2)}) %collective-permute-start) | collective-permute-done | bytes 2097184 | tf_op jit(solution)/shard_map/ppermute | solution.py:28
  74.1 27.6 %collective-permute-done.1 = bf16[8,256,512]{2,1,0:T(8,128)(2,1)S(1)} collective-permute-done((bf16[8,256,512]{2,1,0:T(8,128)(2,1)S(1)}, bf16[8,256,512]{2,1,0:T(8,128)(2,1)S(1)}, u32[]{:S(2)}, u32[]{:S(2)}) %collective-permute-start.1) | collective-permute-done | bytes 2097184 | tf_op jit(solution)/shard_map/ppermute | solution.py:28
  103.0 27.7 %collective-permute-done.2 = bf16[8,256,512]{2,1,0:T(8,128)(2,1)} collective-permute-done((bf16[8,256,512]{2,1,0:T(8,128)(2,1)S(1)}, bf16[8,256,512]{2,1,0:T(8,128)(2,1)}, u32[]{:S(2)}, u32[]{:S(2)}) %collective-permute-start.2) | collective-permute-done | bytes 2097184 | tf_op jit(solution)/shard_map/ppermute | solution.py:28
  131.4 5.2 %all-to-all-start.1 = ((f32[16,8,256]{2,1,0:T(8,128)}), f32[16,8,256]{2,1,0:T(8,128)S(1)}, u32[]{:S(2)}, u32[]{:S(2)}) async-start(f32[16,8,256]{2,1,0:T(8,128)} %broadcast_in_dim.15), calls=%async_computation.1 | async-start | bytes 262144 | tf_op jit(solution)/shard_map/all_to_all | solution.py:17
  136.6 23.2 %collective-permute-done.3 = bf16[8,256,512]{2,1,0:T(8,128)(2,1)} collective-permute-done((bf16[8,256,512]{2,1,0:T(8,128)(2,1)}, bf16[8,256,512]{2,1,0:T(8,128)(2,1)}, u32[]{:S(2)}, u32[]{:S(2)}) %collective-permute-start.3) | collective-permute-done | bytes 2097184 | tf_op jit(solution)/shard_map/ppermute | solution.py:28
  160.0 1.9 copy.19
  161.9 15.7 %gather_fusion = f32[4096,8]{1,0:T(8,128)} fusion(f32[8,4096]{0,1:T(8,128)} %bitcast.105, s32[4096]{0:T(1024)S(1)} %fusion.18), kind=kCustom, calls=%fused_computation | custom fusion | bytes 278528 | tf_op jit(solution)/shard_map/jit(_take)/gather | solution.py:38
  177.7 3.6 %select_rsqrt_fusion = f32[4096,8]{1,0:T(8,128)S(1)} fusion(f32[4096,8]{1,0:T(8,128)} %gather_fusion, pred[4096]{0:T(1024)(128)(4,1)S(1)} %compare_and_fusion), kind=kLoop, calls=%fused_computation.12 | loop fusion | flops 32768 | bytes 266240 | tf_op jit(solution)/shard_map/sqrt | solution.py:38
  183.2 4.4 %collective-permute-done.4 = bf16[8,256,512]{2,1,0:T(8,128)(2,1)} collective-permute-done((bf16[8,256,512]{2,1,0:T(8,128)(2,1)}, bf16[8,256,512]{2,1,0:T(8,128)(2,1)}, u32[]{:S(2)}, u32[]{:S(2)}) %collective-permute-start.4) | collective-permute-done | bytes 2097184 | tf_op jit(solution)/shard_map/ppermute | solution.py:28
  198.1 17.4 %collective-permute-done.5 = bf16[8,256,512]{2,1,0:T(8,128)(2,1)S(1)} collective-permute-done((bf16[8,256,512]{2,1,0:T(8,128)(2,1)}, bf16[8,256,512]{2,1,0:T(8,128)(2,1)S(1)}, u32[]{:S(2)}, u32[]{:S(2)}) %collective-permute-start.5) | collective-permute-done | bytes 2097184 | tf_op jit(solution)/shard_map/ppermute | solution.py:28
  215.4 2.3 fusion.7
  217.8 2.3 fusion.6
  221.6 2.3 fusion.9
  224.0 2.3 fusion.8
  226.3 1.5 maximum_dynamic-update-slice_fusion.4
  227.8 2.3 fusion.10
  230.2 12.8 %collective-permute-done.6 = bf16[8,256,512]{2,1,0:T(8,128)(2,1)S(1)} collective-permute-done((bf16[8,256,512]{2,1,0:T(8,128)(2,1)S(1)}, bf16[8,256,512]{2,1,0:T(8,128)(2,1)S(1)}, u32[]{:S(2)}, u32[]{:S(2)}) %collective-permute-start.6) | collective-permute-done | bytes 2097184 | tf_op jit(solution)/shard_map/ppermute | solution.py:28
  243.0 2.3 fusion.11
  253.2 17.4 %collective-permute-done.7 = bf16[8,256,512]{2,1,0:T(8,128)(2,1)S(1)} collective-permute-done((bf16[8,256,512]{2,1,0:T(8,128)(2,1)S(1)}, bf16[8,256,512]{2,1,0:T(8,128)(2,1)S(1)}, u32[]{:S(2)}, u32[]{:S(2)}) %collective-permute-start.7) | collective-permute-done | bytes 2097184 | tf_op jit(solution)/shard_map/ppermute | solution.py:28
  273.8 24.7 %copy.30 = bf16[8,9,256,512]{3,2,1,0:T(8,128)(2,1)} copy(bf16[8,9,256,512]{2,3,0,1:T(8,128)(2,1)} %maximum_dynamic-update-slice_fusion) | data formatting | bytes 37748736 | tf_op jit(solution)/shard_map/stack | solution.py:61
  (56 shorter events, 27.0 us)
Async XLA Ops:
  43.3 87.5 %copy-start.1 = (f32[8,256]{1,0:T(8,128)S(1)}, f32[8,256]{1,0:T(8,128)}, u32[]{:S(2)}) copy-start(f32[8,256]{1,0:T(8,128)} %param.4) | copy-start | bytes 24580
  43.3 116.5 %copy-start = (s32[4096]{0:T(1024)S(1)}, s32[4096]{0:T(1024)}, u32[]{:S(2)}) copy-start(s32[4096]{0:T(1024)} %param.5) | copy-start | bytes 49156
  46.4 27.6 %collective-permute-start = (bf16[8,256,512]{2,1,0:T(8,128)(2,1)S(1)}, bf16[8,256,512]{2,1,0:T(8,128)(2,1)S(1)}, u32[]{:S(2)}, u32[]{:S(2)}) collective-permute-start(bf16[8,256,512]{2,1,0:T(8,128)(2,1)S(1)} %bitcast.101), channel_id=1, source_target_pairs={{0,1},{1,2},{2,3},{3,4},{4,5},{5,6},{6,7},{7,8},{8,9},{9,10},{10,1... | collective-permute-start | bytes 6291464 | tf_op jit(solution)/shard_map/ppermute | solution.py:28
  74.1 56.6 %copy-start.4 = (bf16[8,256,512]{2,1,0:T(8,128)(2,1)}, bf16[8,256,512]{2,1,0:T(8,128)(2,1)S(1)}, u32[]{:S(2)}) copy-start(bf16[8,256,512]{2,1,0:T(8,128)(2,1)S(1)} %collective-permute-done) | copy-start | bytes 6291460
  74.1 27.6 %collective-permute-start.1 = (bf16[8,256,512]{2,1,0:T(8,128)(2,1)S(1)}, bf16[8,256,512]{2,1,0:T(8,128)(2,1)S(1)}, u32[]{:S(2)}, u32[]{:S(2)}) collective-permute-start(bf16[8,256,512]{2,1,0:T(8,128)(2,1)S(1)} %collective-permute-done), channel_id=1, source_target_pairs={{0,1},{1,2},{2,3},{3,4},{4,5},{5,6},{6,7},{7,8},{8,9},{9,10},{10,1... | collective-permute-start | bytes 6291464 | tf_op jit(solution)/shard_map/ppermute | solution.py:28
  101.6 1.4 copy-start.2
  103.0 27.7 %collective-permute-start.2 = (bf16[8,256,512]{2,1,0:T(8,128)(2,1)S(1)}, bf16[8,256,512]{2,1,0:T(8,128)(2,1)}, u32[]{:S(2)}, u32[]{:S(2)}) collective-permute-start(bf16[8,256,512]{2,1,0:T(8,128)(2,1)S(1)} %collective-permute-done.1), channel_id=1, source_target_pairs={{0,1},{1,2},{2,3},{3,4},{4,5},{5,6},{6,7},{7,8},{8,9},{9,10},{10,1... | collective-permute-start | bytes 6291464 | tf_op jit(solution)/shard_map/ppermute | solution.py:28
  130.7 29.1 %collective-permute-start.3 = (bf16[8,256,512]{2,1,0:T(8,128)(2,1)}, bf16[8,256,512]{2,1,0:T(8,128)(2,1)}, u32[]{:S(2)}, u32[]{:S(2)}) collective-permute-start(bf16[8,256,512]{2,1,0:T(8,128)(2,1)} %collective-permute-done.2), channel_id=1, source_target_pairs={{0,1},{1,2},{2,3},{3,4},{4,5},{5,6},{6,7},{7,8},{8,9},{9,10},{10,1... | collective-permute-start | bytes 6291464 | tf_op jit(solution)/shard_map/ppermute | solution.py:28
  131.4 28.6 %all-to-all-start.1 = ((f32[16,8,256]{2,1,0:T(8,128)}), f32[16,8,256]{2,1,0:T(8,128)S(1)}, u32[]{:S(2)}, u32[]{:S(2)}) async-start(f32[16,8,256]{2,1,0:T(8,128)} %broadcast_in_dim.15), calls=%async_computation.1 | async-start | bytes 262144 | tf_op jit(solution)/shard_map/all_to_all | solution.py:17
  159.8 27.9 %collective-permute-start.4 = (bf16[8,256,512]{2,1,0:T(8,128)(2,1)}, bf16[8,256,512]{2,1,0:T(8,128)(2,1)}, u32[]{:S(2)}, u32[]{:S(2)}) collective-permute-start(bf16[8,256,512]{2,1,0:T(8,128)(2,1)} %collective-permute-done.3), channel_id=1, source_target_pairs={{0,1},{1,2},{2,3},{3,4},{4,5},{5,6},{6,7},{7,8},{8,9},{9,10},{10,1... | collective-permute-start | bytes 6291464 | tf_op jit(solution)/shard_map/ppermute | solution.py:28
  187.7 27.8 %collective-permute-start.5 = (bf16[8,256,512]{2,1,0:T(8,128)(2,1)}, bf16[8,256,512]{2,1,0:T(8,128)(2,1)S(1)}, u32[]{:S(2)}, u32[]{:S(2)}) collective-permute-start(bf16[8,256,512]{2,1,0:T(8,128)(2,1)} %collective-permute-done.4), channel_id=1, source_target_pairs={{0,1},{1,2},{2,3},{3,4},{4,5},{5,6},{6,7},{7,8},{8,9},{9,10},{10,1... | collective-permute-start | bytes 6291464 | tf_op jit(solution)/shard_map/ppermute | solution.py:28
  188.4 2.3 copy-start.5
  192.5 2.3 copy-start.3
  215.4 27.6 %collective-permute-start.6 = (bf16[8,256,512]{2,1,0:T(8,128)(2,1)S(1)}, bf16[8,256,512]{2,1,0:T(8,128)(2,1)S(1)}, u32[]{:S(2)}, u32[]{:S(2)}) collective-permute-start(bf16[8,256,512]{2,1,0:T(8,128)(2,1)S(1)} %collective-permute-done.5), channel_id=1, source_target_pairs={{0,1},{1,2},{2,3},{3,4},{4,5},{5,6},{6,7},{7,8},{8,9},{9,10},{10,1... | collective-permute-start | bytes 6291464 | tf_op jit(solution)/shard_map/ppermute | solution.py:28
  243.0 27.6 %collective-permute-start.7 = (bf16[8,256,512]{2,1,0:T(8,128)(2,1)S(1)}, bf16[8,256,512]{2,1,0:T(8,128)(2,1)S(1)}, u32[]{:S(2)}, u32[]{:S(2)}) collective-permute-start(bf16[8,256,512]{2,1,0:T(8,128)(2,1)S(1)} %collective-permute-done.6), channel_id=1, source_target_pairs={{0,1},{1,2},{2,3},{3,4},{4,5},{5,6},{6,7},{7,8},{8,9},{9,10},{10,1... | collective-permute-start | bytes 6291464 | tf_op jit(solution)/shard_map/ppermute | solution.py:28
where the time goes:
time: 300 us; the launch traced here: 298 us
  waiting for transfers between devices  158 us (53%)
  local copies, waits for them, and re-layouts  58.4 us (19%)
  blocking collectives  34.9 us (12%)
  matrix products  24.4 us (8%)
  other arithmetic  17.1 us (6%)
  starting transfers between devices  5.32 us (2%)
    ppermute x8, waiting for transfers between devices, from_behind(): lax.ppermute(value, axis, [(i, (i + by) % count) for i in range(count)])  158 us
    all_to_all x1, blocking collectives, per_device(): lax.all_to_all(voltages, 'row', split_axis=1, concat_axis=0, tiled=True)  34.9 us
    another operation x1, local copies, waits for them, and re-layouts, per_device(): return jnp.stack(tiles, axis=1)  24.7 us
    gather x1, local copies, waits for them, and re-layouts, per_device(): inverse = 1.0 / jnp.sqrt(jnp.take(autos_all, station_order, axis=1))  15.7 us
    dot_general x9, matrix products, per_device(): jnp.einsum('cih,cjh->cij', own_turned, partner, preferred_element_type=jn...  12.9 us
    unnamed x8, other arithmetic  11.8 us
    dot_general x9, matrix products, per_device(): jnp.einsum('cih,cjh->cij', own_rows, partner, preferred_element_type=jnp....  11.5 us
    unnamed x13, local copies, waits for them, and re-layouts  7.01 us
  transfers between devices with their start and end apart: 9, of which 8 were waited for; matrix products, arithmetic and copies ran while one was open for 19% of the time, Pallas kernels for 0%

commit v1 on v0

v1 whole, which is shorter than its diff:
```python
import functools

import jax
import jax.numpy as jnp
from jax import lax
from jax.experimental import pallas as pl
from jax.experimental.pallas import tpu as pltpu
from jax.sharding import PartitionSpec as P

CHAN = 8
HALF = CHAN // 2
PIECE = 32
BLOCK = 256
WIDE = 512
COLS = 16
TURNED_DOWN = (0, 1)


def comm_kernel(
    x, auto, order, grid, inv, inv_t,
    transit, relay, autos,
    bar_local, s_a2a, s_relay, s_half, s_z, s_y, s_die, s_auto, s_inv,
    r_x, r_o, r_rel, r_blk, r_trans, r_die, r_auto, r_inv,
):
    row = lax.axis_index("row")
    col = lax.axis_index("col")
    xpos, yhi = row // 2, row % 2
    core, ylo = col % 2, (col // 2) % 2
    sib = col + 1 - 2 * core
    ynb = col + 2 - 4 * ylo
    up = (col + 4) % COLS
    down = (col + COLS - 4) % COLS
    is0, is1 = ylo == 0, ylo == 1
    other = 1 - yhi

    def peer_x(d):
        return ((xpos + d) % 4) * 2 + yhi

    def peer_o(d):
        return ((xpos + d) % 4) * 2 + other

    def remote(src, dst, ss, rs, **where):
        return pltpu.make_async_remote_copy(
            src_ref=src, dst_ref=dst, send_sem=ss, recv_sem=rs,
            device_id=where, device_id_type=pl.DeviceIdType.MESH,
        )

    barrier = pltpu.get_barrier_semaphore()
    for d in range(1, 4):
        pl.semaphore_signal(barrier, inc=1, device_id={"row": peer_x(d), "col": col}, device_id_type=pl.DeviceIdType.MESH)
    for d in range(4):
        pl.semaphore_signal(barrier, inc=1, device_id={"row": peer_o(d), "col": ynb}, device_id_type=pl.DeviceIdType.MESH)
    for d in range(1, COLS):
        pl.semaphore_signal(barrier, inc=1, device_id={"row": row, "col": (col + d) % COLS}, device_id_type=pl.DeviceIdType.MESH)
    pl.semaphore_wait(barrier, 3 + 4 + COLS - 1)

    def local_own(ch):
        return pltpu.make_async_copy(x.at[row * CHAN + ch], grid.at[0, ch, xpos, yhi], bar_local.at[ch])

    def a2a_x(ch, d):
        return remote(x.at[peer_x(d) * CHAN + ch], grid.at[0, ch, xpos, yhi], s_a2a.at[ch], r_x.at[ch],
                      row=peer_x(d), col=col)

    def a2a_o(ch, d, first):
        dst = grid.at[2, ch, xpos, yhi] if first else relay.at[ch, xpos]
        return remote(x.at[peer_o(d) * CHAN + ch], dst, s_a2a.at[ch], r_o.at[ch], row=peer_o(d), col=ynb)

    def relayed(ch, first):
        src = relay.at[ch] if first else grid.at[2, ch, :, other]
        return remote(src, grid.at[0, ch, :, other], s_relay.at[ch], r_rel.at[ch], row=row, col=ynb)

    def half(ch):
        return remote(grid.at[0, ch, :, yhi], grid.at[2, ch, :, yhi], s_half.at[ch], r_blk.at[0, ch], row=row, col=ynb)

    def z_send(ch, j, to, target, slot):
        src = transit.at[ch] if j == 6 else grid.at[2 * j, ch]
        if to == 6:
            return remote(src, transit.at[ch], s_z.at[slot, ch], r_trans.at[ch], row=row, col=target)
        return remote(src, grid.at[2 * to, ch], s_z.at[slot, ch], r_blk.at[to - 1, ch], row=row, col=target)

    def y_send(ch, j, to, slot):
        return remote(grid.at[2 * j, ch], grid.at[2 * to, ch], s_y.at[slot, ch], r_blk.at[to - 1, ch], row=row, col=ynb)

    def die(ch, j):
        at = j - core
        return remote(grid.at[2 * j, ch], grid.at[2 * at + 1, ch], s_die.at[at, ch], r_die.at[at, ch], row=row, col=sib)

    def die_start(ch, j):
        if j == 0:
            pl.when(core == 0)(lambda: die(ch, j).start())
        elif j == 4:
            pl.when(core == 1)(lambda: die(ch, j).start())
        else:
            die(ch, j).start()

    def got(sem, ref):
        pltpu.make_async_copy(ref, ref, sem).wait()

    def got_block(j, ch):
        got(r_blk.at[j - 1, ch], grid.at[2 * j, ch])

    def each(count, body):
        lax.fori_loop(0, count, lambda i, carry: (body(i), carry)[1], 0)

    def send_auto(d):
        return remote(auto, autos.at[col], s_auto, r_auto, row=row, col=(col + d) % COLS)

    def exchange(ch):
        local_own(ch).start()
        for d in range(1, 4):
            a2a_x(ch, d).start()
        for d in range(4):
            pl.when(is0)(lambda: a2a_o(ch, d, True).start())
            pl.when(is1)(lambda: a2a_o(ch, d, False).start())

    exchange(0)
    exchange(HALF)
    each(COLS - 1, lambda i: send_auto(i + 1).start())
    autos[pl.ds(col, 1)] = auto[...][None]

    def exchange_pair(i):
        exchange(i + 1)
        exchange(i + 1 + HALF)

    each(HALF - 1, exchange_pair)

    def ready_half(ch):
        got(r_o.at[ch], relay.at[ch])
        pl.when(is0)(lambda: relayed(ch, True).start())
        pl.when(is1)(lambda: relayed(ch, False).start())
        local_own(ch).wait()
        got(r_x.at[ch], x.at[pl.ds(0, 3)])
        pl.when(is0)(lambda: half(ch).start())

    def ready_own_down(ch):
        got(r_rel.at[ch], relay.at[ch])
        z_send(ch, 0, 6, down, 0).start()
        die_start(ch, 0)

    def ready_own_up(ch):
        got(r_rel.at[ch], relay.at[ch])
        z_send(ch, 0, 2, up, 0).start()
        die_start(ch, 0)

    ready_half(0)
    ready_half(HALF)

    def own_pair(i):
        ready_half(i + 1)
        ready_own_down(i)
        ready_half(i + 1 + HALF)
        ready_own_up(i + HALF)

    each(HALF - 1, own_pair)
    ready_own_down(HALF - 1)
    ready_own_up(CHAN - 1)

    got(r_auto, autos.at[pl.ds(0, COLS - 1)])
    mine = order[pl.ds(col, 1), :]

    def gathered(b, total):
        values = autos[pl.ds(b, 1)].reshape(CHAN, BLOCK)
        high = values.astype(jnp.bfloat16)
        rest = values - high.astype(jnp.float32)
        mid = rest.astype(jnp.bfloat16)
        low = (rest - mid.astype(jnp.float32)).astype(jnp.bfloat16)
        stations = lax.broadcasted_iota(jnp.int32, (BLOCK, BLOCK), 0) + b * BLOCK
        hot = jnp.where(stations == mine, 1.0, 0.0).astype(jnp.bfloat16)
        for part in (low, mid, high):
            total = total + jnp.dot(part, hot, preferred_element_type=jnp.float32)
        return total

    values = lax.fori_loop(0, COLS, gathered, jnp.zeros((CHAN, BLOCK), jnp.float32))
    inverse = 1.0 / jnp.sqrt(values)
    inv[0] = inverse
    inv_t[...] = jnp.transpose(inverse)

    def second(i):
        ch = i + HALF
        got(r_trans.at[i], transit.at[i])
        z_send(i, 6, 4, down, 1).start()
        got_block(2, ch)
        z_send(ch, 2, 4, up, 1).start()
        pl.when(is1)(lambda: y_send(ch, 2, 1, 0).start())
        die_start(ch, 2)

        @pl.when(is1)
        def _():
            got(r_blk.at[0, ch], relay.at[ch])
            z_send(ch, 1, 3, up, 2).start()
            die_start(ch, 1)

    each(HALF, second)

    def send_inv(k):
        return remote(inv.at[0], inv.at[k], s_inv, r_inv, row=row, col=(col + k) % COLS)

    for k in range(1, 9):
        send_inv(k).start()

    def third(i):
        ch = i + HALF
        got_block(4, i)
        z_send(i, 4, 2, down, 2).start()
        pl.when(is1)(lambda: y_send(i, 4, 3, 0).start())
        die_start(i, 4)

        @pl.when(is0)
        def _():
            got_block(1, ch)
            z_send(ch, 1, 3, up, 2).start()
            die_start(ch, 1)

        @pl.when(is1)
        def _():
            got(r_blk.at[0, i], relay.at[i])
            die_start(i, 1)

    each(HALF, third)

    def turned_down(i):
        return i < len(TURNED_DOWN)

    def turn(i):
        @pl.when(is0)
        def _():
            got_block(3, i)
            z_send(i, 3, 1, down, 3).start()
            die_start(i, 3)

    each(len(TURNED_DOWN), turn)

    def fourth(i):
        ch = i + HALF
        got_block(2, i)
        pl.when(is0)(lambda: y_send(i, 2, 3, 1).start())
        pl.when(jnp.logical_and(is1, i >= len(TURNED_DOWN)))(lambda: y_send(i, 2, 1, 1).start())
        die_start(i, 2)
        got_block(4, ch)
        die_start(ch, 4)
        got_block(3, ch)
        die_start(ch, 3)

    each(HALF, fourth)

    def last(i):
        @pl.when(is0)
        def _():
            @pl.when(i >= len(TURNED_DOWN))
            def _():
                got_block(3, i)
                die_start(i, 3)
            got_block(1, i)
            die_start(i, 1)

        @pl.when(is1)
        def _():
            got_block(3, i)
            die_start(i, 3)

    each(HALF, last)

    def settle(ch):
        got(s_a2a.at[ch], x.at[pl.ds(0, 7)])
        relayed(ch, True).wait_send()
        pl.when(is0)(lambda: half(ch).wait_send())
        for at in range(4):
            got(r_die.at[at, ch], grid.at[2 * at + 1, ch])
            got(s_die.at[at, ch], grid.at[2 * at + 1, ch])
        for slot in range(3):
            got(s_z.at[slot, ch], grid.at[0, ch])

    each(CHAN, settle)

    def settle_down(i):
        @pl.when(is0)
        def _():
            got(s_y.at[1, i], grid.at[0, i])
            pl.when(turned_down(i))(lambda: got(s_z.at[3, i], grid.at[0, i]))

        @pl.when(is1)
        def _():
            got(s_y.at[0, i], grid.at[0, i])
            got(s_y.at[0, i + HALF], grid.at[0, i])
            pl.when(i >= len(TURNED_DOWN))(lambda: got(s_y.at[1, i], grid.at[0, i]))

    each(HALF, settle_down)
    got(s_auto, autos.at[pl.ds(0, COLS - 1)])
    got(s_inv, inv.at[pl.ds(1, 8)])
    got(r_inv, inv.at[pl.ds(1, 8)])


def tile_kernel(grid, inv, inv_t, out):
    h = pl.program_id(0)
    own = grid[0, 0]
    turned = jnp.concatenate([own[:, BLOCK:], -own[:, :BLOCK]], axis=1)
    lanes = lax.broadcasted_iota(jnp.int32, (BLOCK, CHAN), 1)
    rows = jnp.sum(jnp.where(lanes == h, inv_t[...], 0.0), axis=1, keepdims=True) * (1.0 / BLOCK)
    for k in range(9):
        partner = grid[k, 0]
        factor = rows * inv[k, pl.ds(h, 1), :]
        for half, left in enumerate((own, turned)):
            gram = lax.dot_general(left, partner, (((1,), (1,)), ((), ())), preferred_element_type=jnp.float32)
            out[0, k, :, half * BLOCK:(half + 1) * BLOCK] = (gram * factor).astype(jnp.bfloat16)


def per_device(voltages, auto_prev, station_order):
    x = jnp.transpose(voltages.reshape(PIECE, 64, WIDE), (1, 0, 2))
    order = station_order.reshape(COLS, BLOCK)
    any_space = pl.BlockSpec(memory_space=pl.ANY)
    vmem = pl.BlockSpec(memory_space=pltpu.VMEM)
    dma = pltpu.SemaphoreType.DMA
    grid, inv, inv_t = pl.pallas_call(
        comm_kernel,
        out_shape=(
            jax.ShapeDtypeStruct((9, CHAN, 4, 2, PIECE, WIDE), jnp.bfloat16),
            jax.ShapeDtypeStruct((9, CHAN, BLOCK), jnp.float32),
            jax.ShapeDtypeStruct((BLOCK, CHAN), jnp.float32),
        ),
        in_specs=[any_space, vmem, vmem],
        out_specs=(any_space, vmem, vmem),
        scratch_shapes=[
            pltpu.VMEM((HALF, 4, 2, PIECE, WIDE), jnp.bfloat16),
            pltpu.VMEM((CHAN, 4, PIECE, WIDE), jnp.bfloat16),
            pltpu.VMEM((COLS, CHAN, BLOCK), jnp.float32),
            dma((CHAN,)), dma((CHAN,)), dma((CHAN,)), dma((CHAN,)), dma((4, CHAN)), dma((2, CHAN)), dma((4, CHAN)), dma, dma,
            dma((CHAN,)), dma((CHAN,)), dma((CHAN,)), dma((4, CHAN)), dma((HALF,)), dma((4, CHAN)), dma, dma,
        ],
        compiler_params=pltpu.CompilerParams(collective_id=0, has_side_effects=True),
    )(x, auto_prev, order)
    grid = grid.reshape(9, CHAN, BLOCK, WIDE)
    return pl.pallas_call(
        tile_kernel,
        grid=(CHAN,),
        out_shape=jax.ShapeDtypeStruct((CHAN, 9, BLOCK, WIDE), jnp.bfloat16),
        in_specs=[
            pl.BlockSpec((9, 1, BLOCK, WIDE), lambda h: (0, h, 0, 0)),
            vmem,
            vmem,
        ],
        out_specs=pl.BlockSpec((1, 9, BLOCK, WIDE), lambda h: (h, 0, 0, 0)),
    )(grid, inv, inv_t)


def solution(mesh):
    return jax.shard_map(
        per_device,
        mesh=mesh,
        in_specs=(P(("col", "row"), None, None, None), P("row", "col"), P()),
        out_specs=P("row", None, "col", None),
        check_vma=False,
    )
```

time: 300 us -> 150 us (0.50)
  waiting for transfers between devices: 158 us -> 0 us
  Pallas kernels: 0 us -> 141 us
  local copies, waits for them, and re-layouts: 58.4 us -> 6.96 us
  blocking collectives: 34.9 us -> 0 us
  matrix products: 24.4 us -> 0 us
  other arithmetic: 17.1 us -> 0 us
  starting transfers between devices: 5.32 us -> 0 us
    ppermute x8 -> x0, waiting for transfers between devices: 158 us -> none  [from_behind(): lax.ppermute(value, axis, [(i, (i + by) % count) for i in range(count)])]
    pallas_call x0 -> x2, Pallas kernels: none -> 141 us  [the longest x1 122 us: per_device(): pl.pallas_call(comm_kernel, out_shape=(jax.ShapeDtypeStruct((9, CHAN, 4,...]
    all_to_all x1 -> x0, blocking collectives: 34.9 us -> none  [per_device(): lax.all_to_all(voltages, 'row', split_axis=1, concat_axis=0, tiled=True)]
    another operation x1 -> x0, local copies, waits for them, and re-layouts: 24.7 us -> none  [per_device(): return jnp.stack(tiles, axis=1)]
    dot_general x18 -> x0, matrix products: 24.4 us -> none  [the longest x9 12.9 us: per_device(): jnp.einsum('cih,cjh->cij', own_turned, partner, preferred_element_type=jn...]
    gather x1 -> x0, local copies, waits for them, and re-layouts: 15.7 us -> none  [per_device(): inverse = 1.0 / jnp.sqrt(jnp.take(autos_all, station_order, axis=1))]
    unnamed x8 -> x0, other arithmetic: 11.8 us -> none
    unnamed x13 -> x0, local copies, waits for them, and re-layouts: 7.01 us -> none
  transfers between devices with their start and end apart: 9 -> 0, of which waited for: 8 -> 0; matrix products, arithmetic and copies ran while one was open for 19% -> 0% of each run, Pallas kernels for 0% -> 0%
where the time goes in v1:
time: 150 us; the launch traced here: 148 us
  Pallas kernels  141 us (94%)
  local copies, waits for them, and re-layouts  6.96 us (5%)
    pallas_call x1, Pallas kernels, per_device(): pl.pallas_call(comm_kernel, out_shape=(jax.ShapeDtypeStruct((9, CHAN, 4,...  122 us
    pallas_call x1, Pallas kernels, per_device(): pl.pallas_call(tile_kernel, grid=(CHAN,), out_shape=jax.ShapeDtypeStruct(...  18.7 us
    reshape x2, local copies, waits for them, and re-layouts, per_device(): x = jnp.transpose(voltages.reshape(PIECE, 64, WIDE), (1, 0, 2))  5.63 us

profile of v1, /device:TPU:0, one launch (start us, length us, event | category | flops | bytes accessed | tf_op | source)
XLA Modules:
  0.0 148.1 jit_solution(848051263335703270)
XLA Ops:
  0.0 1.3 reshape.10.order
  1.3 3.2 %reshape.12 = bf16[32,64,512]{2,1,0:T(8,128)(2,1)S(1)} reshape(bf16[32,64,2,256]{3,2,1,0:T(2,128)(2,1)} %param.3) | data formatting | bytes 4194304 | tf_op jit(solution)/shard_map/reshape | solution.py:308
  4.5 2.5 %copy.7 = bf16[32,64,512]{2,0,1:T(8,128)(2,1)} copy(bf16[32,64,512]{2,1,0:T(8,128)(2,1)S(1)} %reshape.12) | data formatting | bytes 4194304 | tf_op jit(solution)/shard_map/reshape | solution.py:308
  7.0 122.4 %shard_map.37 = (bf16[9,8,4,2,32,512]{5,4,3,2,1,0:T(8,128)(2,1)}, f32[9,8,256]{2,1,0:T(8,128)}, f32[256,8]{1,0:T(8,128)}) custom-call(bf16[64,32,512]{2,1,0:T(8,128)(2,1)} %bitcast.5, f32[8,256]{1,0:T(8,128)} %auto.1, s32[16,256]{1,0:T(8,128)} %reshape.10.order), custom_call_target="tpu_custom_call" | custom-call | tf_op jit(solution)/shard_map/pallas_call | solution.py:313
  129.4 18.7 %shard_map.38 = bf16[8,9,256,512]{3,2,1,0:T(8,128)(2,1)} custom-call(bf16[9,8,256,512]{3,2,1,0:T(8,128)(2,1)} %bitcast.4, f32[9,8,256]{2,1,0:T(8,128)} %get-tuple-element.9.inv, f32[256,8]{1,0:T(8,128)} %get-tuple-element.10.inv_t), custom_call_target="tpu_custom_call" | custom-call | tf_op jit(solution)/shard_map/pallas_call | solution.py:332

commit v2 on v1

--- a/solution.py
+++ b/solution.py
@@ -13,6 +13,7 @@
 BLOCK = 256
 WIDE = 512
 COLS = 16
+LAG = 2
 TURNED_DOWN = (0, 1)
 
 
@@ -124,36 +125,55 @@
 
     each(HALF - 1, exchange_pair)
 
-    def ready_half(ch):
+    def own_z(ch, part, falls):
+        src = grid.at[0, ch, :, part]
+        if falls:
+            return remote(src, transit.at[ch, :, part], s_z.at[0, ch], r_trans.at[ch], row=row, col=down)
+        return remote(src, grid.at[4, ch, :, part], s_z.at[0, ch], r_blk.at[1, ch], row=row, col=up)
+
+    def ready_half(ch, falls):
         got(r_o.at[ch], relay.at[ch])
         pl.when(is0)(lambda: relayed(ch, True).start())
         pl.when(is1)(lambda: relayed(ch, False).start())
         local_own(ch).wait()
         got(r_x.at[ch], x.at[pl.ds(0, 3)])
-        pl.when(is0)(lambda: half(ch).start())
-
-    def ready_own_down(ch):
+        own_z(ch, yhi, falls).start()
+
+    def ready_own(ch, falls):
         got(r_rel.at[ch], relay.at[ch])
-        z_send(ch, 0, 6, down, 0).start()
+        own_z(ch, other, falls).start()
         die_start(ch, 0)
 
-    def ready_own_up(ch):
-        got(r_rel.at[ch], relay.at[ch])
-        z_send(ch, 0, 2, up, 0).start()
-        die_start(ch, 0)
-
-    ready_half(0)
-    ready_half(HALF)
-
-    def own_pair(i):
-        ready_half(i + 1)
-        ready_own_down(i)
-        ready_half(i + 1 + HALF)
-        ready_own_up(i + HALF)
-
-    each(HALF - 1, own_pair)
-    ready_own_down(HALF - 1)
-    ready_own_up(CHAN - 1)
+    def second_down(i):
+        got(r_trans.at[i], transit.at[i])
+        z_send(i, 6, 4, down, 1).start()
+
+    def second_up(ch):
+        got_block(2, ch)
+        z_send(ch, 2, 4, up, 1).start()
+        pl.when(is1)(lambda: y_send(ch, 2, 1, 0).start())
+        die_start(ch, 2)
+
+    def step(i):
+        if i < HALF:
+            ready_half(i, True)
+        if 0 <= i - 1 < HALF:
+            ready_own(i - 1, True)
+        if i < HALF:
+            ready_half(i + HALF, False)
+        if 0 <= i - 1 < HALF:
+            ready_own(i - 1 + HALF, False)
+        if 0 <= i - LAG < HALF:
+            second_down(i - LAG)
+            second_up(i - LAG + HALF)
+
+    for i in range(HALF + 1):
+        step(i)
+
+    @pl.when(is0)
+    def _():
+        each(HALF, lambda i: half(i + HALF).start())
+        each(HALF, lambda i: half(i).start())
 
     got(r_auto, autos.at[pl.ds(0, COLS - 1)])
     mine = order[pl.ds(col, 1), :]
@@ -175,22 +195,17 @@
     inv[0] = inverse
     inv_t[...] = jnp.transpose(inverse)
 
-    def second(i):
-        ch = i + HALF
-        got(r_trans.at[i], transit.at[i])
-        z_send(i, 6, 4, down, 1).start()
-        got_block(2, ch)
-        z_send(ch, 2, 4, up, 1).start()
-        pl.when(is1)(lambda: y_send(ch, 2, 1, 0).start())
-        die_start(ch, 2)
-
-        @pl.when(is1)
-        def _():
+    for i in range(HALF + 1, HALF + LAG):
+        step(i)
+
+    @pl.when(is1)
+    def _():
+        def early(i):
+            ch = i + HALF
             got(r_blk.at[0, ch], relay.at[ch])
             z_send(ch, 1, 3, up, 2).start()
             die_start(ch, 1)
-
-    each(HALF, second)
+        each(HALF, early)
 
     def send_inv(k):
         return remote(inv.at[0], inv.at[k], s_inv, r_inv, row=row, col=(col + k) % COLS)
@@ -326,7 +341,7 @@
             dma((CHAN,)), dma((CHAN,)), dma((CHAN,)), dma((CHAN,)), dma((4, CHAN)), dma((2, CHAN)), dma((4, CHAN)), dma, dma,
             dma((CHAN,)), dma((CHAN,)), dma((CHAN,)), dma((4, CHAN)), dma((HALF,)), dma((4, CHAN)), dma, dma,
         ],
-        compiler_params=pltpu.CompilerParams(collective_id=0, has_side_effects=True),
+        compiler_params=pltpu.CompilerParams(collective_id=0, has_side_effects=True, vmem_limit_bytes=8*2**20),
     )(x, auto_prev, order)
     grid = grid.reshape(9, CHAN, BLOCK, WIDE)
     return pl.pallas_call(
@@ -338,7 +353,7 @@
             vmem,
             vmem,
         ],
-        out_specs=pl.BlockSpec((1, 9, BLOCK, WIDE), lambda h: (h, 0, 0, 0)),
+        out_specs=pl.BlockSpec((1, 9, BLOCK, WIDE), lambda h: (h, 0, 0, 0)),compiler_params=pltpu.CompilerParams(vmem_limit_bytes=12*2**20),
     )(grid, inv, inv_t)
 
 

time: 150 us -> 122 us (0.81)
  Pallas kernels: 141 us -> 116 us
  local copies, waits for them, and re-layouts: 6.96 us -> 5.04 us
    pallas_call x1, Pallas kernels: 122 us -> 102 us  [per_device(): pl.pallas_call(comm_kernel, out_shape=(jax.ShapeDtypeStruct((9, CHAN, 4,...]
    pallas_call x1, Pallas kernels: 18.7 us -> 14.2 us  [per_device(): pl.pallas_call(tile_kernel, grid=(CHAN,), out_shape=jax.ShapeDtypeStruct(...]
where the time goes in v2:
time: 122 us; the launch traced here: 121 us
  Pallas kernels  116 us (95%)
  local copies, waits for them, and re-layouts  5.04 us (4%)
    pallas_call x1, Pallas kernels, per_device(): pl.pallas_call(comm_kernel, out_shape=(jax.ShapeDtypeStruct((9, CHAN, 4,...  102 us
    pallas_call x1, Pallas kernels, per_device(): pl.pallas_call(tile_kernel, grid=(CHAN,), out_shape=jax.ShapeDtypeStruct(...  14.2 us
    reshape x2, local copies, waits for them, and re-layouts, per_device(): x = jnp.transpose(voltages.reshape(PIECE, 64, WIDE), (1, 0, 2))  4.31 us

profile of v2, /device:TPU:0, one launch (start us, length us, event | category | flops | bytes accessed | tf_op | source)
XLA Modules:
  0.0 120.8 jit_solution(9678449960151793908)
XLA Ops:
  0.0 0.7 reshape.10.order
  0.7 3.2 %reshape.12 = bf16[32,64,512]{2,1,0:T(8,128)(2,1)S(1)} reshape(bf16[32,64,2,256]{3,2,1,0:T(2,128)(2,1)} %param.3) | data formatting | bytes 4194304 | tf_op jit(solution)/shard_map/reshape | solution.py:323
  3.9 0.0 copy-start
  3.9 1.2 copy.7
  5.1 0.0 copy-done
  5.1 101.6 %shard_map.37 = (bf16[9,8,4,2,32,512]{5,4,3,2,1,0:T(8,128)(2,1)S(1)}, f32[9,8,256]{2,1,0:T(8,128)S(1)}, f32[256,8]{1,0:T(8,128)S(1)}) custom-call(bf16[64,32,512]{2,1,0:T(8,128)(2,1)S(1)} %bitcast.5, f32[8,256]{1,0:T(8,128)S(1)} %copy-done, s32[16,256]{1,0:T(8,128)S(1)} %reshape.10.order), custom_call_target="tpu_custom_call" | custom-call | tf_op jit(solution)/shard_map/pallas_call | solution.py:328
  106.7 14.2 %shard_map.38 = bf16[8,9,256,512]{3,2,1,0:T(8,128)(2,1)} custom-call(bf16[9,8,256,512]{3,2,1,0:T(8,128)(2,1)S(1)} %bitcast.4, f32[9,8,256]{2,1,0:T(8,128)S(1)} %get-tuple-element.9.inv, f32[256,8]{1,0:T(8,128)S(1)} %get-tuple-element.10.inv_t), custom_call_target="tpu_custom_call" | custom-call | tf_op jit(solution)/shard_map/pallas_call | solution.py:347
Async XLA Ops:
  3.9 1.2 copy-start

commit v3 on v1

v3 whole, which is shorter than its diff:
```python
import functools

import jax
import jax.numpy as jnp
from jax import lax
from jax.experimental import pallas as pl
from jax.experimental.pallas import tpu as pltpu
from jax.sharding import PartitionSpec as P

CHAN = 8
HALF = CHAN // 2
PIECE = 32
BLOCK = 256
WIDE = 512
COLS = 16
TURNED_DOWN = (0, 1)
AHEAD = 2.0
FIRST, RATE = 9.0, 3.4
UNIT, DELAY = 5.8, 3.0
INVERT = 26.0
HALVES = 20.0


def plan():
    hops, at = {}, {}
    for n in range(CHAN):
        ch = n // 2 + HALF * (n % 2)
        falls = ch < HALF
        z = "down" if falls else "up"
        for y in (0, 1):
            at["row", ch, y] = FIRST + RATE * n
            hops["relay", ch, y] = ("y", UNIT / 2, [("row", ch, y)])
            hops["near", ch, y] = (z, UNIT / 2, [("row", ch, y)])
            hops["far", ch, y] = (z, UNIT / 2, [("relay", ch, 1 - y)])
            first = [("near", ch, y), ("far", ch, y)]
            if falls:
                hops["64", ch, y] = (z, UNIT, first)
                hops["42", ch, y] = (z, UNIT, [("64", ch, y)])
            else:
                hops["24", ch, y] = (z, UNIT, first)
                hops["13", ch, y] = (z, UNIT, [("y21", ch, 1)] if y == 0 else [("half", ch, 0)])
        hops["half", ch, 0] = ("y", UNIT / 2, [("row", ch, 0)])
        if falls:
            hops["y23", ch, 0] = ("y", UNIT, [("42", ch, 0)])
            hops["y43", ch, 1] = ("y", UNIT, [("64", ch, 1)])
            if ch in TURNED_DOWN:
                hops["31", ch, 0] = (z, UNIT, [("y43", ch, 1)])
            else:
                hops["y21", ch, 1] = ("y", UNIT, [("42", ch, 1)])
        else:
            hops["y21", ch, 1] = ("y", UNIT, [("near", ch, 1), ("far", ch, 1)])
    after = {}
    for name, (_, _, needs) in hops.items():
        for need in needs:
            after.setdefault(need, []).append(name)
    tail = {}

    def left(name):
        if name not in tail:
            tail[name] = hops[name][1] + DELAY + max([left(n) for n in after.get(name, [])], default=0.0)
        return tail[name]

    free, events, waiting = {}, ([], []), dict(hops)
    while waiting:
        best = None
        for name, (link, _, needs) in waiting.items():
            if all(need in at for need in needs):
                ready = max([at[need] for need in needs] + [HALVES if name[0] == "half" else 0.0])
                start = max(ready, free.get((link, name[2]), 0.0))
                key = (round(start, 3), -round(left(name), 3), name)
                if best is None or key < best[0]:
                    best = (key, name, ready, start)
        _, name, ready, start = best
        link, takes, _ = waiting.pop(name)
        free[link, name[2]] = start + takes
        at[name] = start + takes + DELAY
        events[name[2]].append((max(ready, start - AHEAD), name[0], name[1]))
    arrives = {}
    for ch in range(CHAN):
        for y in (0, 1):
            falls = ch < HALF
            arrives[0, ch, y] = at["relay", ch, 1 - y]
            if falls:
                arrives[4, ch, y] = at["64", ch, y]
                arrives[2, ch, y] = at["42", ch, y]
                arrives[3, ch, y] = at["y43", ch, 1] if y == 0 else at["y23", ch, 0]
                turned = ("31", ch, 0) if ch in TURNED_DOWN else ("y21", ch, 1)
                arrives[1, ch, y] = at[turned] if y == 0 else at["half", ch, 0]
            else:
                arrives[2, ch, y] = max(at["near", ch, y], at["far", ch, y])
                arrives[4, ch, y] = at["24", ch, y]
                arrives[3, ch, y] = at["13", ch, y]
                arrives[1, ch, y] = at["y21", ch, 1] if y == 0 else at["half", ch, 0]
            for j in range(1, 5):
                events[y].append((arrives[j, ch, y], "arrived", (j, ch)))
    return tuple(sorted(e, key=lambda item: (item[0], item[1], str(item[2]))) for e in events), arrives


def scaled(own, partner, factor):
    turned = jnp.concatenate([own[:, BLOCK:], -own[:, :BLOCK]], axis=1)
    grams = [
        lax.dot_general(left, partner, (((1,), (1,)), ((), ())), preferred_element_type=jnp.float32)
        for left in (own, turned)
    ]
    return [(gram * factor).astype(jnp.bfloat16) for gram in grams]


def row_factor(inv_t, h):
    lanes = lax.broadcasted_iota(jnp.int32, (BLOCK, CHAN), 1)
    return jnp.sum(jnp.where(lanes == h, inv_t[...], 0.0), axis=1, keepdims=True) * (1.0 / BLOCK)


def comm_kernel(
    x, auto, order, grid, inv, inv_t, ups, downs,
    transit, relay, autos,
    bar_local, s_a2a, s_relay, s_half, s_z, s_y, s_die, s_auto, s_inv,
    r_x, r_o, r_rel, r_blk, r_trans, r_die, r_auto, r_inv,
):
    row = lax.axis_index("row")
    col = lax.axis_index("col")
    xpos, yhi = row // 2, row % 2
    core, ylo = col % 2, (col // 2) % 2
    sib = col + 1 - 2 * core
    ynb = col + 2 - 4 * ylo
    up = (col + 4) % COLS
    down = (col + COLS - 4) % COLS
    is0, is1 = ylo == 0, ylo == 1
    other = 1 - yhi

    def peer_x(d):
        return ((xpos + d) % 4) * 2 + yhi

    def peer_o(d):
        return ((xpos + d) % 4) * 2 + other

    def remote(src, dst, ss, rs, **where):
        return pltpu.make_async_remote_copy(
            src_ref=src, dst_ref=dst, send_sem=ss, recv_sem=rs,
            device_id=where, device_id_type=pl.DeviceIdType.MESH,
        )

    barrier = pltpu.get_barrier_semaphore()
    for d in range(1, 4):
        pl.semaphore_signal(barrier, inc=1, device_id={"row": peer_x(d), "col": col}, device_id_type=pl.DeviceIdType.MESH)
    for d in range(4):
        pl.semaphore_signal(barrier, inc=1, device_id={"row": peer_o(d), "col": ynb}, device_id_type=pl.DeviceIdType.MESH)
    for d in range(1, COLS):
        pl.semaphore_signal(barrier, inc=1, device_id={"row": row, "col": (col + d) % COLS}, device_id_type=pl.DeviceIdType.MESH)
    pl.semaphore_wait(barrier, 3 + 4 + COLS - 1)

    def local_own(ch):
        return pltpu.make_async_copy(x.at[row * CHAN + ch], grid.at[0, ch, xpos, yhi], bar_local.at[ch])

    def a2a_x(ch, d):
        return remote(x.at[peer_x(d) * CHAN + ch], grid.at[0, ch, xpos, yhi], s_a2a.at[ch], r_x.at[ch],
                      row=peer_x(d), col=col)

    def a2a_o(ch, d, first):
        dst = grid.at[2, ch, xpos, yhi] if first else relay.at[ch, xpos]
        return remote(x.at[peer_o(d) * CHAN + ch], dst, s_a2a.at[ch], r_o.at[ch], row=peer_o(d), col=ynb)

    def relayed(ch, first):
        src = relay.at[ch] if first else grid.at[2, ch, :, other]
        return remote(src, grid.at[0, ch, :, other], s_relay.at[ch], r_rel.at[ch], row=row, col=ynb)

    def half(ch):
        return remote(grid.at[0, ch, :, yhi], grid.at[2, ch, :, yhi], s_half.at[ch], r_blk.at[0, ch], row=row, col=ynb)

    def z_send(ch, j, to, target, slot):
        src = transit.at[ch] if j == 6 else grid.at[2 * j, ch]
        if to == 6:
            return remote(src, transit.at[ch], s_z.at[slot, ch], r_trans.at[ch], row=row, col=target)
        return remote(src, grid.at[2 * to, ch], s_z.at[slot, ch], r_blk.at[to - 1, ch], row=row, col=target)

    def y_send(ch, j, to, slot):
        return remote(grid.at[2 * j, ch], grid.at[2 * to, ch], s_y.at[slot, ch], r_blk.at[to - 1, ch], row=row, col=ynb)

    def die(ch, j):
        at = j - core
        return remote(grid.at[2 * j, ch], grid.at[2 * at + 1, ch], s_die.at[at, ch], r_die.at[at, ch], row=row, col=sib)

    def die_start(ch, j):
        if j == 0:
            pl.when(core == 0)(lambda: die(ch, j).start())
        elif j == 4:
            pl.when(core == 1)(lambda: die(ch, j).start())
        else:
            die(ch, j).start()

    def got(sem, ref):
        pltpu.make_async_copy(ref, ref, sem).wait()

    def got_block(j, ch):
        got(r_blk.at[j - 1, ch], grid.at[2 * j, ch])

    def each(count, body):
        lax.fori_loop(0, count, lambda i, carry: (body(i), carry)[1], 0)

    def send_auto(d):
        return remote(auto, autos.at[col], s_auto, r_auto, row=row, col=(col + d) % COLS)

    def exchange(ch):
        local_own(ch).start()
        for d in range(1, 4):
            a2a_x(ch, d).start()
        for d in range(4):
            pl.when(is0)(lambda: a2a_o(ch, d, True).start())
            pl.when(is1)(lambda: a2a_o(ch, d, False).start())

    exchange(0)
    exchange(HALF)
    each(COLS - 1, lambda i: send_auto(i + 1).start())
    autos[pl.ds(col, 1)] = auto[...][None]

    def exchange_pair(i):
        exchange(i + 1)
        exchange(i + 1 + HALF)

    each(HALF - 1, exchange_pair)

    def gathered(b, total):
        mine = order[pl.ds(col, 1), :]
        values = autos[pl.ds(b, 1)].reshape(CHAN, BLOCK)
        high = values.astype(jnp.bfloat16)
        rest = values - high.astype(jnp.float32)
        mid = rest.astype(jnp.bfloat16)
        low = (rest - mid.astype(jnp.float32)).astype(jnp.bfloat16)
        stations = lax.broadcasted_iota(jnp.int32, (BLOCK, BLOCK), 0) + b * BLOCK
        hot = jnp.where(stations == mine, 1.0, 0.0).astype(jnp.bfloat16)
        for part in (low, mid, high):
            total = total + jnp.dot(part, hot, preferred_element_type=jnp.float32)
        return total

    def invert():
        got(r_auto, autos.at[pl.ds(0, COLS - 1)])
        values = lax.fori_loop(0, COLS, gathered, jnp.zeros((CHAN, BLOCK), jnp.float32))
        inverse = 1.0 / jnp.sqrt(values)
        inv[0] = inverse
        inv_t[...] = jnp.transpose(inverse)

    def send_inv(k):
        return remote(inv.at[0], inv.at[k], s_inv, r_inv, row=row, col=(col + k) % COLS)

    def pass_on():
        for k in range(1, 9):
            send_inv(k).start()

    def take_inv():
        got(r_inv, inv.at[pl.ds(1, 8)])

    def own_z(ch, part):
        src = grid.at[0, ch, :, part]
        if ch < HALF:
            return remote(src, transit.at[ch, :, part], s_z.at[0, ch], r_trans.at[ch], row=row, col=down)
        return remote(src, grid.at[4, ch, :, part], s_z.at[0, ch], r_blk.at[1, ch], row=row, col=up)

    seen = (set(), set())

    def once(y, *what):
        if what in seen[y]:
            return False
        seen[y].add(what)
        return True

    def need(y, j, ch):
        if not once(y, "block", j, ch):
            return
        if j == 1 and y == 1:
            need_far(y, ch)
            got(r_blk.at[0, ch], relay.at[ch])
        else:
            got_block(j, ch)
        die_start(ch, j)

    def need_near(y, ch):
        if once(y, "near", ch):
            local_own(ch).wait()
            got(r_x.at[ch], x.at[pl.ds(0, 3)])

    def need_far(y, ch):
        if once(y, "far", ch):
            got(r_o.at[ch], relay.at[ch])

    def need_own(y, ch):
        need_near(y, ch)
        if once(y, "own", ch):
            got(r_rel.at[ch], relay.at[ch])
            die_start(ch, 0)

    def run(y, what, ch):
        if what == "arrived":
            need(y, *ch)
        elif what == "relay":
            need_far(y, ch)
            relayed(ch, y == 0).start()
        elif what == "near":
            need_near(y, ch)
            own_z(ch, yhi).start()
        elif what == "far":
            need_own(y, ch)
            own_z(ch, other).start()
        elif what == "half":
            need_near(y, ch)
            half(ch).start()
        elif what == "64":
            got(r_trans.at[ch], transit.at[ch])
            z_send(ch, 6, 4, down, 1).start()
        elif what in ("42", "24", "13", "31"):
            j, to = int(what[0]), int(what[1])
            need(y, j, ch)
            slot = {"42": 2, "24": 1, "13": 2, "31": 3}[what]
            z_send(ch, j, to, down if ch < HALF else up, slot).start()
        else:
            j, to = int(what[1]), int(what[2])
            need(y, j, ch)
            y_send(ch, j, to, 1 if what == "y23" or (what == "y21" and ch < HALF) else 0).start()

    events, arrives = plan()
    done = [0, 0]

    def until(time, blocks=()):
        for y in (0, 1):
            @pl.when(ylo == y)
            def _(y=y):
                while done[y] < len(events[y]) and events[y][done[y]][0] < time:
                    run(y, *events[y][done[y]][1:])
                    done[y] += 1
                for j, ch in blocks:
                    need_own(y, ch)
                    if j > 0:
                        need(y, j, ch)

    def tiles(first, k):
        def one(i):
            ch = first + i
            if k % 2 == 1:
                got(r_die.at[k // 2, ch], grid.at[k, ch])
            own = grid[0, ch].reshape(BLOCK, WIDE)
            factor = row_factor(inv_t, ch) * inv[k, pl.ds(ch, 1), :]
            for part, value in enumerate(scaled(own, grid[k, ch].reshape(BLOCK, WIDE), factor)):
                lanes = slice(part * BLOCK, (part + 1) * BLOCK)
                if first == 0:
                    downs[i, k // 8, :, lanes] = value
                else:
                    ups[i, k, :, lanes] = value

        each(HALF, one)

    def when_ready(first, k):
        from_blocks = [k // 2] if k % 2 == 0 else [k // 2, k // 2 + 1]
        latest = max(arrives[j, first + i, y] for j in from_blocks for i in range(HALF) for y in (0, 1))
        return latest + (3.0 if k % 2 == 1 else 0.0)

    until(INVERT)
    invert()
    until(INVERT + 2.0)
    pass_on()
    jobs = sorted([(when_ready(HALF, k), HALF, k) for k in range(9)] + [(when_ready(0, k), 0, k) for k in (0, 8)])
    time = INVERT + 6.0
    for index, (ready, first, k) in enumerate(jobs):
        time = max(time, ready)
        until(time, [(k // 2 if k % 2 == 0 else 0, first + i) for i in range(HALF)])
        if index == 0:
            take_inv()
        tiles(first, k)
        time += 1.0
    until(1e9)

    def settle(ch):
        got(s_a2a.at[ch], x.at[pl.ds(0, 7)])
        relayed(ch, True).wait_send()
        pl.when(is0)(lambda: half(ch).wait_send())
        for at in range(4):
            got(s_die.at[at, ch], grid.at[2 * at + 1, ch])
        for slot in range(3):
            got(s_z.at[slot, ch], grid.at[0, ch])

    each(CHAN, settle)

    def settle_down(i):
        @pl.when(is0)
        def _():
            got(s_y.at[1, i], grid.at[0, i])
            pl.when(i < len(TURNED_DOWN))(lambda: got(s_z.at[3, i], grid.at[0, i]))

        @pl.when(is1)
        def _():
            got(s_y.at[0, i], grid.at[0, i])
            got(s_y.at[0, i + HALF], grid.at[0, i])
            pl.when(i >= len(TURNED_DOWN))(lambda: got(s_y.at[1, i], grid.at[0, i]))

        for at in range(4):
            got(r_die.at[at, i], grid.at[2 * at + 1, i])

    each(HALF, settle_down)
    got(s_auto, autos.at[pl.ds(0, COLS - 1)])
    got(s_inv, inv.at[pl.ds(1, 8)])


def finish_kernel(grid, inv, inv_t, ups, downs, out, late, s_up, s_down, s_late):
    copies = [pltpu.make_async_copy(ups.at[i], out.at[HALF + i], s_up.at[i]) for i in range(HALF)]
    for i in range(HALF):
        for at in range(2):
            copies.append(pltpu.make_async_copy(downs.at[i, at], out.at[i, 8 * at], s_down.at[i, at]))
    for copy in copies:
        copy.start()

    def one(ch, carry):
        rows = row_factor(inv_t, ch)
        own = grid[0, ch]
        for k in range(1, 8):
            factor = rows * inv[k, pl.ds(ch, 1), :]
            for part, value in enumerate(scaled(own, grid[k, ch], factor)):
                late[ch, k - 1, :, part * BLOCK:(part + 1) * BLOCK] = value
            pltpu.make_async_copy(late.at[ch, k - 1], out.at[ch, k], s_late.at[ch, k - 1]).start()
        return carry

    lax.fori_loop(0, HALF, one, 0)
    for copy in copies:
        copy.wait()

    def wait(ch, carry):
        for k in range(1, 8):
            pltpu.make_async_copy(late.at[ch, k - 1], out.at[ch, k], s_late.at[ch, k - 1]).wait()
        return carry

    lax.fori_loop(0, HALF, wait, 0)


def per_device(voltages, auto_prev, station_order):
    x = jnp.transpose(voltages.reshape(PIECE, 64, WIDE), (1, 0, 2))
    order = station_order.reshape(COLS, BLOCK)
    any_space = pl.BlockSpec(memory_space=pl.ANY)
    vmem = pl.BlockSpec(memory_space=pltpu.VMEM)
    dma = pltpu.SemaphoreType.DMA
    grid, inv, inv_t, ups, downs = pl.pallas_call(
        comm_kernel,
        out_shape=(
            jax.ShapeDtypeStruct((9, CHAN, 4, 2, PIECE, WIDE), jnp.bfloat16),
            jax.ShapeDtypeStruct((9, CHAN, BLOCK), jnp.float32),
            jax.ShapeDtypeStruct((BLOCK, CHAN), jnp.float32),
            jax.ShapeDtypeStruct((HALF, 9, BLOCK, WIDE), jnp.bfloat16),
            jax.ShapeDtypeStruct((HALF, 2, BLOCK, WIDE), jnp.bfloat16),
        ),
        in_specs=[any_space, vmem, vmem],
        out_specs=(vmem, vmem, vmem, vmem, vmem),
        scratch_shapes=[
            pltpu.VMEM((HALF, 4, 2, PIECE, WIDE), jnp.bfloat16),
            pltpu.VMEM((CHAN, 4, PIECE, WIDE), jnp.bfloat16),
            pltpu.VMEM((COLS, CHAN, BLOCK), jnp.float32),
            dma((CHAN,)), dma((CHAN,)), dma((CHAN,)), dma((CHAN,)), dma((4, CHAN)), dma((2, CHAN)), dma((4, CHAN)), dma, dma,
            dma((CHAN,)), dma((CHAN,)), dma((CHAN,)), dma((4, CHAN)), dma((HALF,)), dma((4, CHAN)), dma, dma,
        ],
        compiler_params=pltpu.CompilerParams(collective_id=0, has_side_effects=True, vmem_limit_bytes=8*2**20),
    )(x, auto_prev, order)
    grid = grid.reshape(9, CHAN, BLOCK, WIDE)
    return pl.pallas_call(
        finish_kernel,
        out_shape=jax.ShapeDtypeStruct((CHAN, 9, BLOCK, WIDE), jnp.bfloat16),
        in_specs=[vmem] * 5,
        out_specs=any_space,
        scratch_shapes=[
            pltpu.VMEM((HALF, 7, BLOCK, WIDE), jnp.bfloat16),
            dma((HALF,)), dma((HALF, 2)), dma((HALF, 7)),
        ],
        compiler_params=pltpu.CompilerParams(vmem_limit_bytes=12 * 2**20),
    )(grid, inv, inv_t, ups, downs)


def solution(mesh):
    return jax.shard_map(
        per_device,
        mesh=mesh,
        in_specs=(P(("col", "row"), None, None, None), P("row", "col"), P()),
        out_specs=P("row", None, "col", None),
        check_vma=False,
    )
```

time: 150 us -> 111 us (0.74)
  Pallas kernels: 141 us -> 105 us
  local copies, waits for them, and re-layouts: 6.96 us -> 5.04 us
    pallas_call x1, Pallas kernels: 122 us -> 98.1 us  [per_device(): pl.pallas_call(comm_kernel, out_shape=(jax.ShapeDtypeStruct((9, CHAN, 4,...]
    pallas_call x1, Pallas kernels: 18.7 us -> 6.78 us  [per_device(): pl.pallas_call(finish_kernel, out_shape=jax.ShapeDtypeStruct((CHAN, 9, BL...]
where the time goes in v3:
time: 111 us; the launch traced here: 110 us
  Pallas kernels  105 us (95%)
  local copies, waits for them, and re-layouts  5.04 us (5%)
    pallas_call x1, Pallas kernels, per_device(): pl.pallas_call(comm_kernel, out_shape=(jax.ShapeDtypeStruct((9, CHAN, 4,...  98.1 us
    pallas_call x1, Pallas kernels, per_device(): pl.pallas_call(finish_kernel, out_shape=jax.ShapeDtypeStruct((CHAN, 9, BL...  6.78 us
    reshape x2, local copies, waits for them, and re-layouts, per_device(): x = jnp.transpose(voltages.reshape(PIECE, 64, WIDE), (1, 0, 2))  4.31 us

profile of v3, /device:TPU:0, one launch (start us, length us, event | category | flops | bytes accessed | tf_op | source)
XLA Modules:
  0.0 110.0 jit_solution(7997616337602226336)
XLA Ops:
  0.0 0.7 reshape.10.order
  0.7 3.2 %reshape.12 = bf16[32,64,512]{2,1,0:T(8,128)(2,1)S(1)} reshape(bf16[32,64,2,256]{3,2,1,0:T(2,128)(2,1)} %param.3) | data formatting | bytes 4194304 | tf_op jit(solution)/shard_map/reshape | solution.py:431
  3.9 0.0 copy-start
  3.9 1.2 %copy.7 = bf16[32,64,512]{2,0,1:T(8,128)(2,1)S(1)} copy(bf16[32,64,512]{2,1,0:T(8,128)(2,1)S(1)} %reshape.12) | data formatting | bytes 4194304 | tf_op jit(solution)/shard_map/reshape | solution.py:431
  5.1 0.0 copy-done
  5.1 98.1 %shard_map.37 = (bf16[9,8,4,2,32,512]{5,4,3,2,1,0:T(8,128)(2,1)S(1)}, f32[9,8,256]{2,1,0:T(8,128)S(1)}, f32[256,8]{1,0:T(8,128)S(1)}, bf16[4,9,256,512]{3,2,1,0:T(8,128)(2,1)S(1)}, bf16[4,2,256,512]{3,2,1,0:T(8,128)(2,1)S(1)}) custom-call(bf16[64,32,512]{2,1,0:T(8,128)(2,1)S(1)} %bitcast.5, f32[8,256]{1,0:T(8,128)S(1)} %copy-done, s32[16,256]{1,0:T(8,128)S(1)} %reshape.10.order), custom_call_target="tpu_custom_call" | custom-call | tf_op jit(solution)/shard_map/pallas_call | solution.py:436
  103.2 6.8 %shard_map.38 = bf16[8,9,256,512]{3,2,1,0:T(8,128)(2,1)} custom-call(bf16[9,8,256,512]{3,2,1,0:T(8,128)(2,1)S(1)} %bitcast.4, f32[9,8,256]{2,1,0:T(8,128)S(1)} %get-tuple-element.11.inv, f32[256,8]{1,0:T(8,128)S(1)} %get-tuple-element.12.inv_t, bf16[4,9,256,512]{3,2,1,0:T(8,128)(2,1)S(1)} %get-tuple-element.13.ups, ...), custom_call_target="tpu_custom_call" | custom-call | tf_op jit(solution)/shard_map/pallas_call | solution.py:457
Async XLA Ops:
  3.9 1.2 %copy-start = (f32[8,256]{1,0:T(8,128)S(1)}, f32[8,256]{1,0:T(8,128)}, u32[]{:S(2)}) copy-start(f32[8,256]{1,0:T(8,128)} %auto.1) | copy-start | bytes 24580

commit v4 on v0

v4 whole, which is shorter than its diff:
```python
import heapq

import jax
import jax.numpy as jnp
from jax import lax
from jax.experimental import pallas as pl
from jax.experimental.pallas import tpu as pltpu
from jax.sharding import PartitionSpec as P

CHAN = 8
EARLY = 5
PIECE = 32
BLOCK = 256
WIDE = 512
COLS = 16
AHEAD = 3.0
FIRST, RATE = 8.0, 3.8
UNIT, DELAY = 2.88, 3.3
DEPTH = 3
INVERT = 26.0
SLOTS = 13
UP, DOWN, ACROSS = 1, 2, 3
TREES = (
    (
        (6, 9, 15, 18, 26),
        (7, 10, 13, 18, 26),
        (6, 10, 15, 18, 26),
        (7, 10, 15, 18, 26),
        (7, 9, 13, 17),
        (7, 11, 13, 17),
        (7, 10, 15, 18, 26),
        (7, 10, 13, 18, 26),
    ),
    (
        (3, 11, 13, 17),
        (3, 11, 13, 17),
        (3, 9, 13, 17),
        (2, 11, 13, 17),
        (3, 9, 13, 17),
        (2, 10, 13, 19, 21),
        (2, 11, 13, 17),
        (3, 11, 13, 17),
    ),
    (
        (11, 13, 19, 22, 30),
        (10, 15, 19, 22, 30),
        (11, 14, 17, 22, 30),
        (11, 13, 17, 22, 30),
        (10, 13, 19, 21),
        (11, 13, 19, 21),
        (11, 13, 17, 21),
        (10, 14, 19, 22, 30),
    ),
    (
        (7, 9, 15, 17, 23),
        (6, 9, 15, 17, 21),
        (7, 9, 15, 17, 23),
        (7, 10, 13, 19, 21),
        (6, 9, 15, 17, 23),
        (7, 10, 13, 19, 22, 30),
        (6, 9, 15, 17, 21),
        (7, 11, 14, 19, 22, 30),
    ),
)


def offset(kind, node):
    return node - (1 if kind >= 2 else 0)


def kept(kind, node):
    return 0 <= offset(kind, node) <= 4


def comes_from(node, link):
    if link == ACROSS:
        return node // 2 * 2 + 1 - node % 2
    step = 6 if link == UP else 2
    return (node + step) % 8


def plan():
    roots = (0, 1, 1, 0)
    children, left = {}, {}
    for kind in range(4):
        for ch in range(CHAN):
            for code in TREES[kind][ch]:
                node, link = code // 4, code % 4
                children.setdefault((kind, ch, comes_from(node, link)), []).append((node, link))

    def rest(kind, ch, node):
        return UNIT + DELAY + max([rest(kind, ch, n) for n, _ in children.get((kind, ch, node), [])], default=0.0)

    queue, busy, heap, at, events = {}, {}, [], {}, ([], [])
    count = 0
    for kind in range(4):
        for ch in range(CHAN):
            heapq.heappush(heap, (FIRST + RATE * ch, count, None, (kind, ch, roots[kind])))
            count += 1
    while heap:
        now, _, line, what = heapq.heappop(heap)
        lines = [line] if line else []
        if what:
            kind, ch, node = what
            at[what] = now
            for to, link in children.get(what, []):
                line = (node % 2, link)
                heapq.heappush(queue.setdefault(line, []), (-rest(kind, ch, to) + DEPTH * ch, count, now, (kind, ch, node, link, to)))
                count += 1
                lines.append(line)
        for line in lines:
            if busy.get(line, 0.0) <= now + 1e-6 and queue.get(line):
                _, _, ready, hop = heapq.heappop(queue[line])
                events[line[0]].append((max(ready, now - AHEAD), count, hop))
                busy[line] = now + UNIT
                heapq.heappush(heap, (now + UNIT + DELAY, count, None, (hop[0], hop[1], hop[4])))
                heapq.heappush(heap, (now + UNIT, count + 1, line, None))
                count += 2
    for (kind, ch, node), time in at.items():
        if kept(kind, node):
            count += 1
            events[node % 2].append((time, count, (kind, ch, node)))
    return tuple(sorted(e) for e in events), at


def scaled(own, partner, factor):
    turned = jnp.concatenate([own[:, BLOCK:], -own[:, :BLOCK]], axis=1)
    grams = [
        lax.dot_general(left, partner, (((1,), (1,)), ((), ())), preferred_element_type=jnp.float32)
        for left in (own, turned)
    ]
    return [(gram * factor).astype(jnp.bfloat16) for gram in grams]


def row_factor(inv_t, h):
    lanes = lax.broadcasted_iota(jnp.int32, (BLOCK, CHAN), 1)
    return jnp.sum(jnp.where(lanes == h, inv_t[...], 0.0), axis=1, keepdims=True) * (1.0 / BLOCK)


def comm_kernel(
    x, auto, order, grid, inv, inv_t, ready_tiles,
    transit, autos, placed,
    s_local, s_a2a, s_hop, s_die, s_auto, s_inv,
    r_x, r_o, r_blk, r_transit, r_die, r_auto, r_inv,
):
    row = lax.axis_index("row")
    col = lax.axis_index("col")
    xpos, yhi = row // 2, row % 2
    core, ylo = col % 2, (col // 2) % 2
    sib = col + 1 - 2 * core
    ynb = col + 2 - 4 * ylo
    up = (col + 4) % COLS
    down = (col + COLS - 4) % COLS
    is0, is1 = ylo == 0, ylo == 1
    other = 1 - yhi

    def peer_x(d):
        return ((xpos + d) % 4) * 2 + yhi

    def peer_o(d):
        return ((xpos + d) % 4) * 2 + other

    def remote(src, dst, ss, rs, **where):
        return pltpu.make_async_remote_copy(
            src_ref=src, dst_ref=dst, send_sem=ss, recv_sem=rs,
            device_id=where, device_id_type=pl.DeviceIdType.MESH,
        )

    barrier = pltpu.get_barrier_semaphore()
    for d in range(1, 4):
        pl.semaphore_signal(barrier, inc=1, device_id={"row": peer_x(d), "col": col}, device_id_type=pl.DeviceIdType.MESH)
    for d in range(4):
        pl.semaphore_signal(barrier, inc=1, device_id={"row": peer_o(d), "col": ynb}, device_id_type=pl.DeviceIdType.MESH)
    for d in range(1, COLS):
        pl.semaphore_signal(barrier, inc=1, device_id={"row": row, "col": (col + d) % COLS}, device_id_type=pl.DeviceIdType.MESH)
    pl.semaphore_wait(barrier, 3 + 4 + COLS - 1)

    parts = (yhi, other)

    def local_own(ch):
        return pltpu.make_async_copy(x.at[row * CHAN + ch], grid.at[0, ch, xpos, yhi], s_local.at[ch])

    def a2a_x(ch, d):
        return remote(x.at[peer_x(d) * CHAN + ch], grid.at[0, ch, xpos, yhi], s_a2a.at[ch], r_x.at[ch],
                      row=peer_x(d), col=col)

    def a2a_o(ch, d, first):
        dst = grid.at[2, ch, xpos, yhi] if first else transit.at[1, ch, xpos, yhi]
        return remote(x.at[peer_o(d) * CHAN + ch], dst, s_a2a.at[ch], r_o.at[ch], row=peer_o(d), col=ynb)

    def place(kind, ch, node):
        if kept(kind, node):
            return grid.at[2 * offset(kind, node), ch, :, parts[kind % 2]]
        return transit.at[kind // 2, ch, :, parts[kind % 2]]

    def arrival(kind, ch, node):
        if kept(kind, node):
            return r_blk.at[kind % 2, offset(kind, node), ch]
        return r_transit.at[kind // 2, kind % 2, ch]

    def hop(kind, ch, node, link, to, slot):
        where = {"row": row, "col": {UP: up, DOWN: down, ACROSS: ynb}[link]}
        return remote(place(kind, ch, node), place(kind, ch, to), s_hop.at[slot, ch], arrival(kind, ch, to), **where)

    def die(ch, j, part):
        at = j - core
        return remote(grid.at[2 * j, ch, :, part], grid.at[2 * at + 1, ch, :, part], s_die.at[at, ch], r_die.at[at, ch],
                      row=row, col=sib)

    def die_start(ch, j, part):
        if j == 0:
            pl.when(core == 0)(lambda: die(ch, j, part).start())
        elif j == 4:
            pl.when(core == 1)(lambda: die(ch, j, part).start())
        else:
            die(ch, j, part).start()

    def got(sem, ref):
        pltpu.make_async_copy(ref, ref, sem).wait()

    def each(count, body):
        lax.fori_loop(0, count, lambda i, carry: (body(i), carry)[1], 0)

    def send_auto(d):
        return remote(auto, autos.at[col], s_auto, r_auto, row=row, col=(col + d) % COLS)

    def exchange(ch):
        local_own(ch).start()
        for d in range(1, 4):
            a2a_x(ch, d).start()
        for d in range(4):
            pl.when(is0)(lambda: a2a_o(ch, d, True).start())
            pl.when(is1)(lambda: a2a_o(ch, d, False).start())

    exchange(0)
    each(COLS - 1, lambda i: send_auto(i + 1).start())
    own_auto = pltpu.make_async_copy(auto, autos.at[col], s_local.at[CHAN])
    own_auto.start()
    own_order = pltpu.make_async_copy(order, placed, s_local.at[CHAN + 1])
    own_order.start()

    each(CHAN - 1, lambda i: exchange(i + 1))

    def gathered(b, total):
        mine = placed[pl.ds(pl.multiple_of(col * BLOCK, BLOCK), BLOCK)].reshape(1, BLOCK)
        values = autos[pl.ds(b, 1)].reshape(CHAN, BLOCK)
        high = values.astype(jnp.bfloat16)
        rest = values - high.astype(jnp.float32)
        mid = rest.astype(jnp.bfloat16)
        low = (rest - mid.astype(jnp.float32)).astype(jnp.bfloat16)
        stations = lax.broadcasted_iota(jnp.int32, (BLOCK, BLOCK), 0) + b * BLOCK
        hot = jnp.where(stations == mine, 1.0, 0.0).astype(jnp.bfloat16)
        for part in (low, mid, high):
            total = total + jnp.dot(part, hot, preferred_element_type=jnp.float32)
        return total

    def invert():
        got(r_auto, autos.at[pl.ds(0, COLS - 1)])
        own_auto.wait()
        own_order.wait()
        values = lax.fori_loop(0, COLS, gathered, jnp.zeros((CHAN, BLOCK), jnp.float32))
        inverse = 1.0 / jnp.sqrt(values)
        inv[0] = inverse
        inv_t[...] = jnp.transpose(inverse)

    def send_inv(k):
        return remote(inv.at[0], inv.at[k], s_inv, r_inv, row=row, col=(col + k) % COLS)

    def pass_on():
        for k in range(1, 9):
            send_inv(k).start()

    def take_inv():
        got(r_inv, inv.at[pl.ds(1, 8)])

    events, arrives = plan()
    seen, done, sent = (set(), set()), [0, 0], ([], [])

    def need(y, kind, ch, node):
        if (kind, ch, node) in seen[y]:
            return
        seen[y].add((kind, ch, node))
        part = parts[kind % 2]
        if kind == (0, 2)[y] and node == y:
            local_own(ch).wait()
            got(r_x.at[ch], x.at[pl.ds(0, 3)])
        elif kind == (3, 1)[y] and node == y:
            got(r_o.at[ch], transit.at[0, ch, :, 0])
        else:
            got(arrival(kind, ch, node), transit.at[0, ch, :, 0])
        if kept(kind, node):
            die_start(ch, offset(kind, node), part)

    def until(time, channel=None):
        for y in (0, 1):
            @pl.when(ylo == y)
            def _(y=y):
                while done[y] < len(events[y]) and events[y][done[y]][0] < time:
                    what = events[y][done[y]][2]
                    done[y] += 1
                    need(y, *what[:3])
                    if len(what) > 3:
                        slot = len([ch for ch, _ in sent[y] if ch == what[1]])
                        sent[y].append((what[1], slot))
                        hop(*what, slot).start()
                if channel is not None:
                    for kind, ch, node in sorted(arrives):
                        if ch == channel and node % 2 == y and kept(kind, node):
                            need(y, kind, ch, node)

    def tiles(ch, first, count):
        own = grid[0, ch].reshape(BLOCK, WIDE)
        rows = row_factor(inv_t, ch)

        def one(i):
            k = first + i
            factor = rows * inv[k, ch:ch + 1, :]
            for part, value in enumerate(scaled(own, grid[k, ch].reshape(BLOCK, WIDE), factor)):
                ready_tiles[ch, k, :, part * BLOCK:(part + 1) * BLOCK] = value

        each(count, one)

    until(INVERT)
    invert()
    until(INVERT + 2.0)
    pass_on()
    time = INVERT + 6.0
    for ch in range(EARLY):
        time = max(time, 3.0 + max(t for (kind, c, node), t in arrives.items() if c == ch and kept(kind, node)))
        until(time, ch)
        if ch == 0:
            take_inv()
        for at in range(4):
            got(r_die.at[at, ch], grid.at[2 * at + 1, ch])
        for first in (0, 3, 6):
            until(time)
            tiles(ch, first, 3)
            time += 0.7
    until(1e9)

    def settle(ch):
        got(s_a2a.at[ch], x.at[pl.ds(0, 7)])
        for at in range(4):
            got(s_die.at[at, ch], grid.at[2 * at + 1, ch])

    each(CHAN, settle)
    for ch in range(EARLY, CHAN):
        for at in range(4):
            got(r_die.at[at, ch], grid.at[2 * at + 1, ch])
    for y in (0, 1):
        @pl.when(ylo == y)
        def _(y=y):
            for ch, slot in sent[y]:
                got(s_hop.at[slot, ch], transit.at[0, ch, :, 0])
    got(s_auto, autos.at[pl.ds(0, COLS - 1)])
    got(s_inv, inv.at[pl.ds(1, 8)])


def finish_kernel(grid, inv, inv_t, ready_tiles, out, late, s_ready, s_late):
    copies = [pltpu.make_async_copy(ready_tiles.at[i], out.at[i], s_ready.at[i]) for i in range(EARLY)]
    for copy in copies:
        copy.start()

    def write(i, k):
        return pltpu.make_async_copy(late.at[i, k], out.at[EARLY + i, k], s_late.at[i, k])

    def one(i, carry):
        rows = row_factor(inv_t, EARLY + i)
        own = grid[0, EARLY + i]
        for k in range(9):
            factor = rows * inv[k, pl.ds(EARLY + i, 1), :]
            for part, value in enumerate(scaled(own, grid[k, EARLY + i], factor)):
                late[i, k, :, part * BLOCK:(part + 1) * BLOCK] = value
            write(i, k).start()
        return carry

    lax.fori_loop(0, CHAN - EARLY, one, 0)
    for copy in copies:
        copy.wait()

    def wait(i, carry):
        for k in range(9):
            write(i, k).wait()
        return carry

    lax.fori_loop(0, CHAN - EARLY, wait, 0)


def per_device(voltages, auto_prev, station_order):
    x = jnp.transpose(voltages.reshape(PIECE, 64, WIDE), (1, 0, 2))
    in_hbm = pl.BlockSpec(memory_space=pltpu.HBM)
    any_space = pl.BlockSpec(memory_space=pl.ANY)
    vmem = pl.BlockSpec(memory_space=pltpu.VMEM)
    dma = pltpu.SemaphoreType.DMA
    grid, inv, inv_t, ready_tiles = pl.pallas_call(
        comm_kernel,
        out_shape=(
            jax.ShapeDtypeStruct((9, CHAN, 4, 2, PIECE, WIDE), jnp.bfloat16),
            jax.ShapeDtypeStruct((9, CHAN, BLOCK), jnp.float32),
            jax.ShapeDtypeStruct((BLOCK, CHAN), jnp.float32),
            jax.ShapeDtypeStruct((EARLY, 9, BLOCK, WIDE), jnp.bfloat16),
        ),
        in_specs=[any_space, in_hbm, in_hbm],
        out_specs=(vmem, vmem, vmem, vmem),
        scratch_shapes=[
            pltpu.VMEM((2, CHAN, 4, 2, PIECE, WIDE), jnp.bfloat16),
            pltpu.VMEM((COLS, CHAN, BLOCK), jnp.float32),
            pltpu.VMEM((COLS * BLOCK,), jnp.int32),
            dma((CHAN + 2,)), dma((CHAN,)), dma((SLOTS, CHAN)), dma((4, CHAN)), dma, dma,
            dma((CHAN,)), dma((CHAN,)), dma((2, 5, CHAN)), dma((2, 2, CHAN)), dma((4, CHAN)), dma, dma,
        ],
        compiler_params=pltpu.CompilerParams(collective_id=0, has_side_effects=True, vmem_limit_bytes=10 * 2**20),
    )(x, *(pltpu.with_memory_space_constraint(a, pltpu.HBM) for a in (auto_prev, station_order)))
    grid = grid.reshape(9, CHAN, BLOCK, WIDE)
    return pl.pallas_call(
        finish_kernel,
        out_shape=jax.ShapeDtypeStruct((CHAN, 9, BLOCK, WIDE), jnp.bfloat16),
        in_specs=[vmem] * 4,
        out_specs=any_space,
        scratch_shapes=[
            pltpu.VMEM((CHAN - EARLY, 9, BLOCK, WIDE), jnp.bfloat16),
            dma((EARLY,)), dma((CHAN - EARLY, 9)),
        ],
        compiler_params=pltpu.CompilerParams(vmem_limit_bytes=12 * 2**20),
    )(grid, inv, inv_t, ready_tiles)


def solution(mesh):
    return jax.shard_map(
        per_device,
        mesh=mesh,
        in_specs=(P(("col", "row"), None, None, None), P("row", "col"), P()),
        out_specs=P("row", None, "col", None),
        check_vma=False,
    )
```

time: 300 us -> 105 us (0.35)
  waiting for transfers between devices: 158 us -> 0 us
  Pallas kernels: 0 us -> 99.7 us
  local copies, waits for them, and re-layouts: 58.4 us -> 4.31 us
  blocking collectives: 34.9 us -> 0 us
  matrix products: 24.4 us -> 0 us
  other arithmetic: 17.1 us -> 0 us
  starting transfers between devices: 5.32 us -> 0 us
    ppermute x8 -> x0, waiting for transfers between devices: 158 us -> none  [from_behind(): lax.ppermute(value, axis, [(i, (i + by) % count) for i in range(count)])]
    pallas_call x0 -> x2, Pallas kernels: none -> 99.7 us  [the longest x1 93 us: per_device(): pl.pallas_call(comm_kernel, out_shape=(jax.ShapeDtypeStruct((9, CHAN, 4,...]
    all_to_all x1 -> x0, blocking collectives: 34.9 us -> none  [per_device(): lax.all_to_all(voltages, 'row', split_axis=1, concat_axis=0, tiled=True)]
    another operation x1 -> x0, local copies, waits for them, and re-layouts: 24.7 us -> none  [per_device(): return jnp.stack(tiles, axis=1)]
    dot_general x18 -> x0, matrix products: 24.4 us -> none  [the longest x9 12.9 us: per_device(): jnp.einsum('cih,cjh->cij', own_turned, partner, preferred_element_type=jn...]
    gather x1 -> x0, local copies, waits for them, and re-layouts: 15.7 us -> none  [per_device(): inverse = 1.0 / jnp.sqrt(jnp.take(autos_all, station_order, axis=1))]
    unnamed x8 -> x0, other arithmetic: 11.8 us -> none
    unnamed x13 -> x0, local copies, waits for them, and re-layouts: 7.01 us -> none
  transfers between devices with their start and end apart: 9 -> 0, of which waited for: 8 -> 0; matrix products, arithmetic and copies ran while one was open for 19% -> 0% of each run, Pallas kernels for 0% -> 0%
where the time goes in v4:
time: 105 us; the launch traced here: 104 us
  Pallas kernels  99.7 us (95%)
  local copies, waits for them, and re-layouts  4.31 us (4%)
    pallas_call x1, Pallas kernels, per_device(): pl.pallas_call(comm_kernel, out_shape=(jax.ShapeDtypeStruct((9, CHAN, 4,...  93 us
    pallas_call x1, Pallas kernels, per_device(): pl.pallas_call(finish_kernel, out_shape=jax.ShapeDtypeStruct((CHAN, 9, BL...  6.71 us
    reshape x2, local copies, waits for them, and re-layouts, per_device(): x = jnp.transpose(voltages.reshape(PIECE, 64, WIDE), (1, 0, 2))  4.31 us

profile of v4, /device:TPU:0, one launch (start us, length us, event | category | flops | bytes accessed | tf_op | source)
XLA Modules:
  0.0 104.0 jit_solution(1001762376749323277)
XLA Ops:
  0.0 3.2 %reshape.8 = bf16[32,64,512]{2,1,0:T(8,128)(2,1)S(1)} reshape(bf16[32,64,2,256]{3,2,1,0:T(2,128)(2,1)} %param.3) | data formatting | bytes 4194304 | tf_op jit(solution)/shard_map/reshape | solution.py:390
  3.2 1.2 %copy.7 = bf16[32,64,512]{2,0,1:T(8,128)(2,1)S(1)} copy(bf16[32,64,512]{2,1,0:T(8,128)(2,1)S(1)} %reshape.8) | data formatting | bytes 4194304 | tf_op jit(solution)/shard_map/reshape | solution.py:390
  4.3 93.0 %shard_map.37 = (bf16[9,8,4,2,32,512]{5,4,3,2,1,0:T(8,128)(2,1)S(1)}, f32[9,8,256]{2,1,0:T(8,128)S(1)}, f32[256,8]{1,0:T(8,128)S(1)}, bf16[5,9,256,512]{3,2,1,0:T(8,128)(2,1)S(1)}) custom-call(bf16[64,32,512]{2,1,0:T(8,128)(2,1)S(1)} %bitcast.5, f32[8,256]{1,0:T(8,128)} %auto.1, s32[4096]{0:T(1024)} %order.1), custom_call_target="tpu_custom_call" | custom-call | tf_op jit(solution)/shard_map/pallas_call | solution.py:395
  97.3 6.7 %shard_map.38 = bf16[8,9,256,512]{3,2,1,0:T(8,128)(2,1)} custom-call(bf16[9,8,256,512]{3,2,1,0:T(8,128)(2,1)S(1)} %bitcast.4, f32[9,8,256]{2,1,0:T(8,128)S(1)} %get-tuple-element.10.inv, f32[256,8]{1,0:T(8,128)S(1)} %get-tuple-element.11.inv_t, bf16[5,9,256,512]{3,2,1,0:T(8,128)(2,1)S(1)} %get-tuple-element.12.ready_tiles), custom_call_target="tpu_custom_call" | custom-call | tf_op jit(solution)/shard_map/pallas_call | solution.py:415

commit v5 on v4

--- a/solution.py
+++ b/solution.py
@@ -8,7 +8,7 @@
 from jax.sharding import PartitionSpec as P
 
 CHAN = 8
-EARLY = 5
+EARLY = 4
 PIECE = 32
 BLOCK = 256
 WIDE = 512

time: 105 us -> 106 us (level)
  no operation moved by 1% of the time
where the time goes in v5:
time: 106 us; the launch traced here: 104 us
  Pallas kernels  99.8 us (94%)
  local copies, waits for them, and re-layouts  4.31 us (4%)
    pallas_call x1, Pallas kernels, per_device(): pl.pallas_call(comm_kernel, out_shape=(jax.ShapeDtypeStruct((9, CHAN, 4,...  93 us
    pallas_call x1, Pallas kernels, per_device(): pl.pallas_call(finish_kernel, out_shape=jax.ShapeDtypeStruct((CHAN, 9, BL...  6.79 us
    reshape x2, local copies, waits for them, and re-layouts, per_device(): x = jnp.transpose(voltages.reshape(PIECE, 64, WIDE), (1, 0, 2))  4.31 us

profile of v5, /device:TPU:0, one launch (start us, length us, event | category | flops | bytes accessed | tf_op | source)
XLA Modules:
  0.0 104.1 jit_solution(11004272924033835375)
XLA Ops:
  0.0 3.2 %reshape.8 = bf16[32,64,512]{2,1,0:T(8,128)(2,1)S(1)} reshape(bf16[32,64,2,256]{3,2,1,0:T(2,128)(2,1)} %param.3) | data formatting | bytes 4194304 | tf_op jit(solution)/shard_map/reshape | solution.py:390
  3.2 1.2 %copy.7 = bf16[32,64,512]{2,0,1:T(8,128)(2,1)S(1)} copy(bf16[32,64,512]{2,1,0:T(8,128)(2,1)S(1)} %reshape.8) | data formatting | bytes 4194304 | tf_op jit(solution)/shard_map/reshape | solution.py:390
  4.3 93.0 %shard_map.37 = (bf16[9,8,4,2,32,512]{5,4,3,2,1,0:T(8,128)(2,1)S(1)}, f32[9,8,256]{2,1,0:T(8,128)S(1)}, f32[256,8]{1,0:T(8,128)S(1)}, bf16[4,9,256,512]{3,2,1,0:T(8,128)(2,1)S(1)}) custom-call(bf16[64,32,512]{2,1,0:T(8,128)(2,1)S(1)} %bitcast.5, f32[8,256]{1,0:T(8,128)} %auto.1, s32[4096]{0:T(1024)} %order.1), custom_call_target="tpu_custom_call" | custom-call | tf_op jit(solution)/shard_map/pallas_call | solution.py:395
  97.3 6.8 %shard_map.38 = bf16[8,9,256,512]{3,2,1,0:T(8,128)(2,1)} custom-call(bf16[9,8,256,512]{3,2,1,0:T(8,128)(2,1)S(1)} %bitcast.4, f32[9,8,256]{2,1,0:T(8,128)S(1)} %get-tuple-element.10.inv, f32[256,8]{1,0:T(8,128)S(1)} %get-tuple-element.11.inv_t, bf16[4,9,256,512]{3,2,1,0:T(8,128)(2,1)S(1)} %get-tuple-element.12.ready_tiles), custom_call_target="tpu_custom_call" | custom-call | tf_op jit(solution)/shard_map/pallas_call | solution.py:415
